TPU v7x, 32 devices: a whole 2x2x4 slice. The times are simulated.
32 devices in a mesh: af: 16 (over z, y, x), sa: 2 (over core).
Axes of the slice: x: 2, y: 2, z: 4, core: 2. Of those that a mesh axis runs over, the one named last changes fastest.
Arguments:
- series: float32 [8, 262144], P('sa', 'af'), parts along dimension 0, may hold values from -48 to 48
- tapers: float32 [10, 262144], P(None, 'af'), may hold values from -16 to 16
- concentration: float32 [10], replicated, may hold values from 0.2 to 0.95
- qi_weights: float32 [4, 10, 10], replicated, may hold values from -0.625 to 0.625
Outputs:
- spectrum: float32 [8, 16, 16384], P('sa', 'af'), parts along dimension 0
- qi_terms: float32 [8, 4, 16, 16384], P('sa', None, 'af'), parts along dimension 0
There are 2 independent parts, one for each index of `sa`. A program takes and returns all parts, laid end to end along the dimension named above; an argument that names none is the same for every part. Nothing has to cross between parts.
All inputs are finite; a program needn't handle non-finite values.
Results may differ from a plain program's by a relative error of at most 0.0001.
Values sent between devices are 32-bit elements; how exact they have to be, the bound alone decides.
A program may use at most 128 MiB of HBM per device.

v0:
```python
import math

import jax
import jax.numpy as jnp
from jax import lax
from jax.sharding import PartitionSpec as P

ITERS = 3


def fourier_table(length):
    indices = jnp.arange(length, dtype=jnp.int32)
    product = indices[:, None] * indices[None, :] % length
    angles = product.astype(jnp.float32) * (2.0 * math.pi / length)
    return (jnp.cos(angles), jnp.sin(angles))


def spectral_mean(estimate, length_all):
    return lax.psum(jnp.sum(estimate, axis=1), "af") / length_all


def local(series, tapers, concentration, qi_weights):
    highest = lax.Precision.HIGHEST
    shards = lax.axis_size("af")
    device_rank = lax.axis_index("af")
    series_count, local_len = series.shape
    taper_count = tapers.shape[0]
    block_len = local_len // shards
    length_all = local_len * shards
    unit_scale = 1.0 / math.sqrt(length_all)
    scaled = series * unit_scale
    got_series, got_tapers = (
        lax.all_to_all(
            scaled.reshape(series_count, shards, block_len),
            "af",
            split_axis=1,
            concat_axis=1,
            tiled=True,
        ),
        lax.all_to_all(
            tapers.reshape(taper_count, shards, block_len),
            "af",
            split_axis=1,
            concat_axis=1,
            tiled=True,
        ),
    )
    tapered = got_tapers[None] * got_series[:, None]
    cos_dev, sin_dev = fourier_table(shards)
    first_re = jnp.einsum("skpb,pc->skcb", tapered, cos_dev, precision=highest)
    first_im = -jnp.einsum("skpb,pc->skcb", tapered, sin_dev, precision=highest)
    sample_pos = device_rank * block_len + jnp.arange(block_len, dtype=jnp.int32)
    sample_phase = jnp.arange(shards, dtype=jnp.int32)[:, None] * sample_pos[None, :] % length_all
    angles = sample_phase.astype(jnp.float32) * (2.0 * math.pi / length_all)
    twist_cos = jnp.cos(angles)
    twist_sin = jnp.sin(angles)
    turned_re = first_re * twist_cos + first_im * twist_sin
    turned_im = first_im * twist_cos - first_re * twist_sin
    recv_re, recv_im = (
        lax.all_to_all(turned_re, "af", split_axis=2, concat_axis=2, tiled=True),
        lax.all_to_all(turned_im, "af", split_axis=2, concat_axis=2, tiled=True),
    )
    second_re = jnp.einsum("skrb,rc->skcb", recv_re, cos_dev, precision=highest) + jnp.einsum(
        "skrb,rc->skcb", recv_im, sin_dev, precision=highest
    )
    second_im = jnp.einsum("skrb,rc->skcb", recv_im, cos_dev, precision=highest) - jnp.einsum(
        "skrb,rc->skcb", recv_re, sin_dev, precision=highest
    )
    inner_phase = (
        jnp.arange(shards, dtype=jnp.int32)[:, None]
        * jnp.arange(block_len, dtype=jnp.int32)[None, :]
        % local_len
    )
    inner_angles = inner_phase.astype(jnp.float32) * (2.0 * math.pi / local_len)
    inner_cos = jnp.cos(inner_angles)
    inner_sin = jnp.sin(inner_angles)
    bent_re = second_re * inner_cos + second_im * inner_sin
    bent_im = second_im * inner_cos - second_re * inner_sin
    cos_blk, sin_blk = fourier_table(block_len)
    spec_re = jnp.einsum("skcb,bd->skdc", bent_re, cos_blk, precision=highest) + jnp.einsum(
        "skcb,bd->skdc", bent_im, sin_blk, precision=highest
    )
    spec_im = jnp.einsum("skcb,bd->skdc", bent_im, cos_blk, precision=highest) - jnp.einsum(
        "skcb,bd->skdc", bent_re, sin_blk, precision=highest
    )
    spec_re = spec_re.reshape(series_count, taper_count, local_len)
    spec_im = spec_im.reshape(series_count, taper_count, local_len)
    powers = spec_re * spec_re + spec_im * spec_im
    qi_list = []
    for term_index in range(qi_weights.shape[0]):
        mixed_re = jnp.einsum("jk,skf->sjf", qi_weights[term_index], spec_re, precision=highest)
        mixed_im = jnp.einsum("jk,skf->sjf", qi_weights[term_index], spec_im, precision=highest)
        qi_list.append(jnp.sum(spec_re * mixed_re + spec_im * mixed_im, axis=1))
    qi_terms = jnp.stack(qi_list, axis=1)
    retained = concentration[None, :, None]
    estimate = 0.5 * (powers[:, 0] + powers[:, 1])
    for sweep_index in range(ITERS):
        variance = spectral_mean(estimate, length_all)
        weight = (
            retained
            / (retained * estimate[:, None, :] + (1.0 - retained) * variance[:, None, None]) ** 2
        )
        estimate = jnp.sum(weight * powers, axis=1) / jnp.sum(weight, axis=1)
    return (
        estimate.reshape(series_count, 1, local_len),
        qi_terms.reshape(series_count, qi_terms.shape[1], 1, local_len),
    )


def solution(mesh):
    placed = (P("sa", "af"), P(None, "af"), P(), P())
    return jax.shard_map(
        local,
        mesh=mesh,
        in_specs=placed,
        out_specs=(P("sa", "af", None), P("sa", None, "af", None)),
        check_vma=False,
    )
```

profile of v0, /device:TPU:0, one launch (start us, length us, event | category | flops | bytes accessed | tf_op | source)
XLA Modules:
  0.0 598.7 jit_solution(10614809215614160121)
XLA Ops:
  2.3 8.3 %all-to-all-start.1 = ((f32[4,16,1024]{2,0,1:T(4,128)}), f32[4,16,1024]{2,0,1:T(4,128)S(1)}, u32[]{:S(2)}, u32[]{:S(2)}) async-start(f32[4,16,1024]{2,0,1:T(4,128)} %bitcast.5), calls=%async_computation.1 | async-start | bytes 524288 | tf_op jit(solution)/shard_map/all_to_all | solution.py:33
  14.0 6.6 %all-to-all-done.1 = f32[4,16,1024]{2,0,1:T(4,128)S(1)} async-done(((f32[4,16,1024]{2,0,1:T(4,128)}), f32[4,16,1024]{2,0,1:T(4,128)S(1)}, u32[]{:S(2)}, u32[]{:S(2)}) %all-to-all-start.1) | async-done | bytes 262176 | tf_op jit(solution)/shard_map/all_to_all | solution.py:33
  20.6 3.7 all-to-all-start
  24.7 23.2 %all-to-all-done = f32[10,16,1024]{2,0,1:T(8,128)S(1)} async-done(((f32[10,16,1024]{2,0,1:T(8,128)}), f32[10,16,1024]{2,0,1:T(8,128)S(1)}, u32[]{:S(2)}, u32[]{:S(2)}) %all-to-all-start) | async-done | bytes 655392 | tf_op jit(solution)/shard_map/all_to_all | solution.py:40
  48.3 2.5 fusion.34
  50.8 4.5 add_bitcast_fusion.1
  55.3 3.2 copy.155
  58.5 5.9 all-to-all-start.3
  64.4 5.0 copy.153
  69.3 45.9 %all-to-all-done.3 = f32[4,10,16,1024]{3,0,1,2:T(4,128)S(1)} async-done(((f32[4,10,16,1024]{3,0,1,2:T(4,128)}), f32[4,10,16,1024]{3,0,1,2:T(4,128)S(1)}, u32[]{:S(2)}, u32[]{:S(2)}) %all-to-all-start.3) | async-done | bytes 2621472 | tf_op jit(solution)/shard_map/all_to_all | solution.py:61
  115.2 12.3 %all-to-all-start.2 = ((f32[4,10,16,1024]{3,0,1,2:T(4,128)}), f32[4,10,16,1024]{3,0,1,2:T(4,128)}, u32[]{:S(2)}, u32[]{:S(2)}) async-start(f32[4,10,16,1024]{3,0,1,2:T(4,128)} %copy.153), calls=%async_computation.2 | async-start | bytes 5242880 | tf_op jit(solution)/shard_map/all_to_all | solution.py:60
  127.8 5.0 fusion.45
  132.9 5.1 fusion.47
  138.0 40.8 %all-to-all-done.2 = f32[4,10,16,1024]{3,0,1,2:T(4,128)} async-done(((f32[4,10,16,1024]{3,0,1,2:T(4,128)}), f32[4,10,16,1024]{3,0,1,2:T(4,128)}, u32[]{:S(2)}, u32[]{:S(2)}) %all-to-all-start.2) | async-done | bytes 2621472 | tf_op jit(solution)/shard_map/all_to_all | solution.py:60
  178.8 6.1 %fusion.70 = f32[16,4,10,1024]{3,0,2,1:T(8,128)S(1)} fusion(f32[16,4,10,1024]{3,0,2,1:T(8,128)} %fusion.45, f32[4,10,16,1024]{3,0,1,2:T(4,128)} %all-to-all-done.2), kind=kOutput, calls=%fused_computation.81 | convolution fusion | flops 126488064 | bytes 7864320 | tf_op jit(solution)/shard_map/skrb,rc->skcb/dot_general | solution.py:66
  185.0 17.2 %fusion.67 = f32[16,4,10,1024]{3,0,2,1:T(8,128)S(1)} fusion(f32[16,4,10,1024]{3,0,2,1:T(8,128)S(1)} %copy-done.3, f32[4,10,16,1024]{3,0,1,2:T(4,128)} %all-to-all-done.2), kind=kOutput, calls=%fused_computation.80 | convolution fusion | flops 126488064 | bytes 7864320 | tf_op jit(solution)/shard_map/skrb,rc->skcb/dot_general | solution.py:63
  202.1 25.0 %fusion.23 = f32[1024,4,10,16]{0,3,2,1:T(8,128)S(1)} fusion(f32[16,4,10,1024]{3,0,2,1:T(8,128)S(1)} %fusion.70, f32[16,4,10,1024]{3,0,2,1:T(8,128)S(1)} %fusion.67, f32[16,1024]{1,0:T(8,128)S(1)} %get-tuple-element.26, f32[16,1024]{1,0:T(8,128)S(1)} %get-tuple-element.27), kind=kOutput, calls=%fused_computation.34 | convolution fusion | flops 8069709824 | bytes 7995392 | tf_op jit(solution)/shard_map/skcb,bd->skdc/dot_general | solution.py:83
  227.1 25.3 %fusion.25 = f32[1024,4,10,16]{0,3,2,1:T(8,128)} fusion(f32[16,4,10,1024]{3,0,2,1:T(8,128)S(1)} %fusion.67, f32[16,4,10,1024]{3,0,2,1:T(8,128)S(1)} %fusion.70, f32[16,1024]{1,0:T(8,128)S(1)} %get-tuple-element.26, f32[16,1024]{1,0:T(8,128)S(1)} %get-tuple-element.27), kind=kOutput, calls=%fused_computation.36 | convolution fusion | flops 8069709824 | bytes 7995392 | tf_op jit(solution)/shard_map/skcb,bd->skdc/dot_general | solution.py:80
  252.5 24.6 %subtract_bitcast_fusion = f32[4,10,1024,16]{2,3,1,0:T(8,128)S(1)} fusion(f32[1024,4,10,16]{0,3,2,1:T(8,128)S(1)} %fusion.23, f32[16,4,10,1024]{3,0,2,1:T(8,128)S(1)} %fusion.67, f32[16,4,10,1024]{3,0,2,1:T(8,128)S(1)} %fusion.70, f32[16,1024]{1,0:T(8,128)S(1)} %get-tuple-element.26, f32[16,1024]{1,0:T(8,128)S(1)} %get-tuple-element.27), kind=kOutput, calls=%fused_computation.64 | convolution fusion | flops 8070365184 | bytes 10616832 | tf_op jit(solution)/shard_map/skcb,bd->skdc/dot_general | solution.py:83
  277.1 10.1 %copy.160 = f32[4,10,1024,16]{3,2,0,1:T(8,128)} copy(f32[4,10,1024,16]{2,3,1,0:T(8,128)S(1)} %subtract_bitcast_fusion) | data formatting | bytes 5242880 | tf_op jit(solution)/shard_map/sub | solution.py:83
  287.2 16.1 %reshape.261 = f32[4,10,16384]{2,0,1:T(4,128)} reshape(f32[4,10,1024,16]{3,2,0,1:T(8,128)} %copy.160) | data formatting | bytes 5242880 | tf_op jit(solution)/shard_map/reshape | solution.py:87
  303.3 27.8 %add_bitcast_fusion = f32[4,10,1024,16]{2,3,1,0:T(8,128)S(1)} fusion(f32[1024,4,10,16]{0,3,2,1:T(8,128)} %fusion.25, f32[16,4,10,1024]{3,0,2,1:T(8,128)} %copy-done.4, f32[16,4,10,1024]{3,0,2,1:T(8,128)} %copy-done.5, f32[16,1024]{1,0:T(8,128)S(1)} %get-tuple-element.26, f32[16,1024]{1,0:T(8,128)S(1)} %get-tuple-element.27), kind=kOutput, calls=%fused_computation.65 | convolution fusion | flops 8070365184 | bytes 10616832 | tf_op jit(solution)/shard_map/skcb,bd->skdc/dot_general | solution.py:80
  332.6 10.1 %copy.159 = f32[4,10,1024,16]{3,2,0,1:T(8,128)} copy(f32[4,10,1024,16]{2,3,1,0:T(8,128)S(1)} %add_bitcast_fusion) | data formatting | bytes 5242880 | tf_op jit(solution)/shard_map/add | solution.py:80
  342.7 14.9 %reshape.260 = f32[4,10,16384]{2,0,1:T(4,128)S(1)} reshape(f32[4,10,1024,16]{3,2,0,1:T(8,128)} %copy.159) | data formatting | bytes 5242880 | tf_op jit(solution)/shard_map/reshape | solution.py:86
  359.9 46.9 %psum.21 = f32[4]{0:T(128)S(1)} all-reduce(f32[4]{0:T(128)S(1)} %get-tuple-element.16), channel_id=1, replica_groups=mesh['af'=16,'sa'=2] {'af'}, use_global_device_ids=true, to_apply=%region_1.2 | all-reduce | flops 4 | bytes 32 | tf_op jit(solution)/shard_map/psum | solution.py:19
  406.8 2.0 mul.486
  408.9 2.2 copy.161
  411.2 3.5 multiply_reduce_fusion.2
  416.6 3.4 reduce_sum.133
  421.3 2.0 reduce_sum.132
  425.2 36.6 %psum.22 = f32[4]{0:T(128)S(1)} all-reduce(f32[4]{0:T(128)S(1)} %get-tuple-element.14), channel_id=1, replica_groups=mesh['af'=16,'sa'=2] {'af'}, use_global_device_ids=true, to_apply=%region_5.6 | all-reduce | flops 4 | bytes 32 | tf_op jit(solution)/shard_map/psum | solution.py:19
  461.9 2.2 copy.163
  464.2 3.5 multiply_reduce_fusion.1
  469.6 2.7 reduce_sum.138
  472.3 2.3 fusion.43
  474.6 2.0 reduce_sum.137
  477.5 38.8 %psum.23 = f32[4]{0:T(128)S(1)} all-reduce(f32[4]{0:T(128)S(1)} %get-tuple-element.12), channel_id=1, replica_groups=mesh['af'=16,'sa'=2] {'af'}, use_global_device_ids=true, to_apply=%region_9.10 | all-reduce | flops 4 | bytes 32 | tf_op jit(solution)/shard_map/psum | solution.py:19
  516.4 2.2 copy.166
  518.7 3.5 multiply_reduce_fusion
  524.1 2.7 reduce_sum.141
  529.2 7.3 %fusion.2 = f32[4,10,16384]{2,1,0:T(8,128)S(1)} fusion(f32[4,10,16384]{2,0,1:T(4,128)S(1)} %reshape.260, f32[1,10,10]{2,0,1:T(1,128)S(1)} %get-tuple-element.23), kind=kOutput, calls=%fused_computation.4 | convolution fusion | flops 79298560 | bytes 5243280 | tf_op jit(solution)/shard_map/jk,skf->sjf/dot_general | solution.py:91
  536.6 9.1 %fusion.82 = f32[4,16384]{1,0:T(4,128)S(1)} fusion(f32[4,10,16384]{2,1,0:T(8,128)S(1)} %fusion.2, f32[4,10,16384]{2,0,1:T(4,128)S(1)} %copy-done, f32[1,10,10]{2,0,1:T(1,128)S(1)} %get-tuple-element.23), kind=kOutput, calls=%fused_computation.85 | convolution fusion | flops 80543744 | bytes 5505424 | tf_op jit(solution)/shard_map/jk,skf->sjf/dot_general | solution.py:92
  545.9 7.3 %fusion.5 = f32[4,10,16384]{2,1,0:T(8,128)S(1)} fusion(f32[4,10,16384]{2,0,1:T(4,128)S(1)} %reshape.260, f32[1,10,10]{2,0,1:T(1,128)S(1)} %get-tuple-element.21), kind=kOutput, calls=%fused_computation.9 | convolution fusion | flops 79298560 | bytes 5243280 | tf_op jit(solution)/shard_map/jk,skf->sjf/dot_general | solution.py:91
  553.3 8.9 %fusion.79 = f32[4,16384]{1,0:T(4,128)S(1)} fusion(f32[4,10,16384]{2,1,0:T(8,128)S(1)} %fusion.5, f32[4,10,16384]{2,0,1:T(4,128)S(1)} %copy-done, f32[1,10,10]{2,0,1:T(1,128)S(1)} %get-tuple-element.21), kind=kOutput, calls=%fused_computation.84 | convolution fusion | flops 80543744 | bytes 5505424 | tf_op jit(solution)/shard_map/jk,skf->sjf/dot_general | solution.py:92
  562.4 7.3 %fusion.8 = f32[4,10,16384]{2,1,0:T(8,128)S(1)} fusion(f32[4,10,16384]{2,0,1:T(4,128)S(1)} %reshape.260, f32[1,10,10]{2,0,1:T(1,128)S(1)} %get-tuple-element.22), kind=kOutput, calls=%fused_computation.14 | convolution fusion | flops 79298560 | bytes 5243280 | tf_op jit(solution)/shard_map/jk,skf->sjf/dot_general | solution.py:91
  569.7 8.9 %fusion.76 = f32[4,16384]{1,0:T(4,128)S(1)} fusion(f32[4,10,16384]{2,1,0:T(8,128)S(1)} %fusion.8, f32[4,10,16384]{2,0,1:T(4,128)S(1)} %copy-done, f32[1,10,10]{2,0,1:T(1,128)S(1)} %get-tuple-element.22), kind=kOutput, calls=%fused_computation.83 | convolution fusion | flops 80543744 | bytes 5505424 | tf_op jit(solution)/shard_map/jk,skf->sjf/dot_general | solution.py:92
  578.8 7.3 %fusion.11 = f32[4,10,16384]{2,1,0:T(8,128)S(1)} fusion(f32[4,10,16384]{2,0,1:T(4,128)S(1)} %reshape.260, f32[1,10,10]{2,0,1:T(1,128)S(1)} %get-tuple-element.20), kind=kOutput, calls=%fused_computation.19 | convolution fusion | flops 79298560 | bytes 5243280 | tf_op jit(solution)/shard_map/jk,skf->sjf/dot_general | solution.py:91
  586.2 9.0 %fusion.73 = f32[4,16384]{1,0:T(4,128)S(1)} fusion(f32[4,10,16384]{2,1,0:T(8,128)S(1)} %fusion.11, f32[4,10,16384]{2,0,1:T(4,128)S(1)} %copy-done, f32[1,10,10]{2,0,1:T(1,128)S(1)} %get-tuple-element.20), kind=kOutput, calls=%fused_computation.82 | convolution fusion | flops 80543744 | bytes 5505424 | tf_op jit(solution)/shard_map/jk,skf->sjf/dot_general | solution.py:92
  (57 shorter events, 26.5 us)
Async XLA Ops:
  2.3 18.2 %all-to-all-start.1 = ((f32[4,16,1024]{2,0,1:T(4,128)}), f32[4,16,1024]{2,0,1:T(4,128)S(1)}, u32[]{:S(2)}, u32[]{:S(2)}) async-start(f32[4,16,1024]{2,0,1:T(4,128)} %bitcast.5), calls=%async_computation.1 | async-start | bytes 524288 | tf_op jit(solution)/shard_map/all_to_all | solution.py:33
  20.6 27.3 %all-to-all-start = ((f32[10,16,1024]{2,0,1:T(8,128)}), f32[10,16,1024]{2,0,1:T(8,128)S(1)}, u32[]{:S(2)}, u32[]{:S(2)}) async-start(f32[10,16,1024]{2,0,1:T(8,128)} %copy.150), calls=%async_computation | async-start | bytes 2097152 | tf_op jit(solution)/shard_map/all_to_all | solution.py:40
  58.5 56.7 %all-to-all-start.3 = ((f32[4,10,16,1024]{3,0,1,2:T(4,128)}), f32[4,10,16,1024]{3,0,1,2:T(4,128)S(1)}, u32[]{:S(2)}, u32[]{:S(2)}) async-start(f32[4,10,16,1024]{3,0,1,2:T(4,128)} %copy.155), calls=%async_computation.3 | async-start | bytes 5242880 | tf_op jit(solution)/shard_map/all_to_all | solution.py:61
  69.3 58.5 %copy-start.8 = (f32[10]{0:T(128)S(1)}, f32[10]{0:T(128)}, u32[]{:S(2)}) copy-start(f32[10]{0:T(128)} %param.6) | copy-start | bytes 124
  69.3 58.5 %copy-start.7 = (f32[4,10,10]{2,0,1:T(4,128)S(1)}, f32[4,10,10]{2,0,1:T(4,128)}, u32[]{:S(2)}) copy-start(f32[4,10,10]{2,0,1:T(4,128)} %param.7) | copy-start | bytes 4804
  115.2 63.6 %all-to-all-start.2 = ((f32[4,10,16,1024]{3,0,1,2:T(4,128)}), f32[4,10,16,1024]{3,0,1,2:T(4,128)}, u32[]{:S(2)}, u32[]{:S(2)}) async-start(f32[4,10,16,1024]{3,0,1,2:T(4,128)} %copy.153), calls=%async_computation.2 | async-start | bytes 5242880 | tf_op jit(solution)/shard_map/all_to_all | solution.py:60
  138.0 47.0 %copy-start.3 = (f32[16,4,10,1024]{3,0,2,1:T(8,128)S(1)}, f32[16,4,10,1024]{3,0,2,1:T(8,128)}, u32[]{:S(2)}) copy-start(f32[16,4,10,1024]{3,0,2,1:T(8,128)} %fusion.47) | copy-start | bytes 7864324
  184.9 67.5 %copy-start.4 = (f32[16,4,10,1024]{3,0,2,1:T(8,128)}, f32[16,4,10,1024]{3,0,2,1:T(8,128)S(1)}, u32[]{:S(2)}) copy-start(f32[16,4,10,1024]{3,0,2,1:T(8,128)S(1)} %fusion.70) | copy-start | bytes 7864324
  202.1 50.3 %copy-start.5 = (f32[16,4,10,1024]{3,0,2,1:T(8,128)}, f32[16,4,10,1024]{3,0,2,1:T(8,128)S(1)}, u32[]{:S(2)}) copy-start(f32[16,4,10,1024]{3,0,2,1:T(8,128)S(1)} %fusion.67) | copy-start | bytes 7864324
  277.1 10.2 %copy-start.1 = (f32[4,10,1024,16]{2,3,1,0:T(8,128)}, f32[4,10,1024,16]{2,3,1,0:T(8,128)S(1)}, u32[]{:S(2)}) copy-start(f32[4,10,1024,16]{2,3,1,0:T(8,128)S(1)} %subtract_bitcast_fusion) | copy-start | bytes 7864324
  331.1 1.5 copy-start.2
  522.1 4.7 copy-start.6
  529.2 7.3 %copy-start = (f32[4,10,16384]{2,0,1:T(4,128)S(1)}, f32[4,10,16384]{2,0,1:T(4,128)}, u32[]{:S(2)}) copy-start(f32[4,10,16384]{2,0,1:T(4,128)} %reshape.261) | copy-start | bytes 7864324
where the time goes:
time: 608 us; the launch traced here: 599 us
  matrix products  208 us (34%)
  blocking collectives  122 us (20%)
  waiting for transfers between devices  116 us (19%)
  local copies, waits for them, and re-layouts  95.8 us (16%)
  starting transfers between devices  30.2 us (5%)
  other arithmetic  24.1 us (4%)
    psum x3, blocking collectives, spectral_mean(): return lax.psum(jnp.sum(estimate, axis=1), 'af') / length_all  122 us
    all_to_all x1, waiting for transfers between devices, local(): lax.all_to_all(turned_im, 'af', split_axis=2, concat_axis=2, tiled=True)  45.9 us
    all_to_all x1, waiting for transfers between devices, local(): lax.all_to_all(turned_re, 'af', split_axis=2, concat_axis=2, tiled=True)  40.8 us
    dot_general x4, matrix products, local(): jnp.einsum('jk,skf->sjf', qi_weights[term_index], spec_im, precision=high...  35.9 us
    dot_general x4, matrix products, local(): jnp.einsum('jk,skf->sjf', qi_weights[term_index], spec_re, precision=high...  29.4 us
    dot_general x1, matrix products, local(): jnp.einsum('skcb,bd->skdc', bent_re, cos_blk, precision=highest)  27.8 us
    dot_general x1, matrix products, local(): jnp.einsum('skcb,bd->skdc', bent_im, sin_blk, precision=highest)  25.3 us
    dot_general x1, matrix products, local(): jnp.einsum('skcb,bd->skdc', bent_re, sin_blk, precision=highest)  25 us
  transfers between devices with their start and end apart: 4, of which 4 were waited for; matrix products, arithmetic and copies ran while one was open for 3% of the time, Pallas kernels for 0%

commit v1 on v0

v1 whole, which is shorter than its diff:
```python
import functools
import math

import jax
import jax.numpy as jnp
import numpy as np
from jax import lax
from jax.experimental import pallas as pl
from jax.experimental.pallas import tpu as pltpu
from jax.sharding import PartitionSpec as P

ITERS = 3
LANES = 128
CHUNK = 16


def add(a, b):
    if a is None:
        return b
    return a if b is None else a + b


def sub(a, b):
    if b is None:
        return a
    return -b if a is None else a - b


def butterfly(values):
    n = len(values)
    if n == 1:
        return values
    even, odd = butterfly(values[0::2]), butterfly(values[1::2])
    low, high = [], []
    for k in range(n // 2):
        (er, ei), (tr, ti) = even[k], odd[k]
        if 4 * k == n:
            tr, ti = ti, (None if tr is None else -tr)
        elif k:
            c, s = math.cos(2 * math.pi * k / n), math.sin(2 * math.pi * k / n)
            if ti is None:
                tr, ti = tr * c, tr * (-s)
            else:
                tr, ti = tr * c + ti * s, ti * c - tr * s
        low.append((add(er, tr), add(ei, ti)))
        high.append((sub(er, tr), sub(ei, ti)))
    return low + high


def front_kernel(series_ref, tapers_ref, twist_ref, out_ref):
    shards, tapers = tapers_ref.shape[0], tapers_ref.shape[1]

    def body(k, carry):
        got = [(series_ref[p, 0] * tapers_ref[p, k], None) for p in range(shards)]
        for q, (re, im) in enumerate(butterfly(got)):
            c, s = twist_ref[0, q], twist_ref[1, q]
            if im is None:
                out_ref[q, 0, 0, k], out_ref[q, 1, 0, k] = re * c, re * (-s)
            else:
                out_ref[q, 0, 0, k] = re * c + im * s
                out_ref[q, 1, 0, k] = im * c - re * s
        return carry

    lax.fori_loop(0, tapers, body, 0)


def split(x):
    high = x.astype(jnp.bfloat16)
    return high, (x - high.astype(jnp.float32)).astype(jnp.bfloat16)


def dot3(a, b):
    dot = functools.partial(jnp.dot, preferred_element_type=jnp.float32)
    return dot(a[0], b[0]) + (dot(a[0], b[1]) + dot(a[1], b[0]))


def refine(estimate, powers, keep, variance):
    top = bottom = None
    for k, power in enumerate(powers):
        base = keep[k] * estimate + (1.0 - keep[k]) * variance
        weight = keep[k] / (base * base)
        top = add(top, weight * power)
        bottom = add(bottom, weight)
    return top / bottom


def back_kernel(keep_ref, pair_ref, var_ref, recv_ref, left_ref, right_ref, inner_ref,
                power_ref, est_ref, qi_ref, spec, qi):
    tapers = recv_ref.shape[3]
    rows = spec.shape[2]
    terms = qi.shape[0]
    left = (left_ref[0], left_ref[1])
    right = (right_ref[0], right_ref[1])

    def transform(k, carry):
        re = recv_ref[:, 0, 0, k].reshape(rows, LANES)
        im = recv_ref[:, 1, 0, k].reshape(rows, LANES)
        mid = dot3(left, split(jnp.concatenate([re, im], axis=0)))
        mr, mi = mid[:rows], mid[rows:]
        c, s = inner_ref[0], inner_ref[1]
        turned = jnp.concatenate([mr * c + mi * s, mi * c - mr * s], axis=1)
        done = dot3(split(turned), right)
        spec[0, k] = done[:, :LANES]
        spec[1, k] = done[:, LANES:]
        return carry

    lax.fori_loop(0, tapers, transform, 0)
    variance = var_ref[pl.program_id(0)]
    keep = [keep_ref[k] for k in range(tapers)]

    def combine(i, carry):
        at = pl.ds(pl.multiple_of(i * CHUNK, CHUNK), CHUNK)
        re = [spec[0, k, at] for k in range(tapers)]
        im = [spec[1, k, at] for k in range(tapers)]
        sums = [None] * terms
        powers = []
        pair = 0
        for j in range(tapers):
            for k in range(j, tapers):
                both = re[j] * re[k] + im[j] * im[k]
                if j == k:
                    powers.append(both)
                    power_ref[0, j, at] = both
                for t in range(terms):
                    sums[t] = add(sums[t], pair_ref[t, pair] * both)
                pair += 1
        for t in range(terms):
            qi[t, at] = sums[t]
        est_ref[0, at] = refine(0.5 * (powers[0] + powers[1]), powers, keep, variance)
        return carry

    lax.fori_loop(0, rows // CHUNK, combine, 0)
    for t in range(terms):
        qi_ref[0, t] = qi[t].T


def sweep_kernel(last, keep_ref, var_ref, power_ref, est_ref, out_ref, hold):
    tapers, rows = power_ref.shape[1], power_ref.shape[2]
    variance = var_ref[pl.program_id(0)]
    keep = [keep_ref[k] for k in range(tapers)]

    def body(i, carry):
        at = pl.ds(pl.multiple_of(i * CHUNK, CHUNK), CHUNK)
        powers = [power_ref[0, k, at] for k in range(tapers)]
        hold[at] = refine(est_ref[0, at], powers, keep, variance)
        return carry

    lax.fori_loop(0, rows // CHUNK, body, 0)
    out_ref[0] = hold[...].T if last else hold[...]


def whole(shape):
    return pl.BlockSpec(shape, lambda i: (0,) * len(shape))


def each(shape, axis):
    return pl.BlockSpec(shape, lambda i: tuple(i if d == axis else 0 for d in range(len(shape))))


def smem():
    return pl.BlockSpec(memory_space=pltpu.SMEM)


def complex_table(n, left):
    angle = 2 * np.pi * (np.outer(np.arange(n), np.arange(n)) % n) / n
    c, s = np.cos(angle), np.sin(angle)
    full = np.block([[c, s], [-s, c]])
    full = jnp.asarray((full if left else full.T).astype(np.float32))
    return jnp.stack(split(full))


def phase(a, b, modulus):
    angles = (a * b % modulus).astype(jnp.float32) * (2.0 * math.pi / modulus)
    return jnp.stack([jnp.cos(angles), jnp.sin(angles)])


def local(series, tapers, concentration, qi_weights):
    shards = lax.axis_size("af")
    rank = lax.axis_index("af")
    count, local_len = series.shape
    taper_count = tapers.shape[0]
    terms = qi_weights.shape[0]
    block_len = local_len // shards
    sub_rows = block_len // LANES
    rows = local_len // LANES
    length_all = local_len * shards
    f32 = jnp.float32

    both = jnp.concatenate([series * (1.0 / math.sqrt(length_all)), tapers], axis=0)
    both = both.reshape(count + taper_count, shards, sub_rows, LANES).transpose(1, 0, 2, 3)
    got = lax.all_to_all(both, "af", split_axis=0, concat_axis=0, tiled=True)
    got_series, got_tapers = got[:, :count], got[:, count:]

    first = jnp.sum((got_series * got_tapers[:, :1]) ** 2, axis=(0, 2, 3))
    second = jnp.sum((got_series * got_tapers[:, 1:2]) ** 2, axis=(0, 2, 3))
    variance = lax.psum(0.5 * (first + second), "af")

    pos = rank * block_len + jnp.arange(block_len, dtype=jnp.int32)
    twist = phase(jnp.arange(shards, dtype=jnp.int32)[:, None], pos[None, :], length_all)
    twist = twist.reshape(2, shards, sub_rows, LANES)
    turned = pl.pallas_call(
        front_kernel,
        grid=(count,),
        out_shape=jax.ShapeDtypeStruct((shards, 2, count, taper_count, sub_rows, LANES), f32),
        in_specs=[
            each((shards, 1, sub_rows, LANES), 1),
            whole((shards, taper_count, sub_rows, LANES)),
            whole((2, shards, sub_rows, LANES)),
        ],
        out_specs=each((shards, 2, 1, taper_count, sub_rows, LANES), 2),
    )(got_series, got_tapers, twist)
    recv = lax.all_to_all(turned, "af", split_axis=0, concat_axis=0, tiled=True)

    inner = phase(
        jnp.arange(rows, dtype=jnp.int32)[:, None],
        jnp.arange(LANES, dtype=jnp.int32)[None, :],
        local_len,
    )
    symmetric = qi_weights + qi_weights.transpose(0, 2, 1)
    pairs = jnp.stack(
        [
            qi_weights[:, j, j] if j == k else symmetric[:, j, k]
            for j in range(taper_count)
            for k in range(j, taper_count)
        ],
        axis=1,
    )
    plane = (1, rows, LANES)
    flat = (1, LANES, rows)
    powers, estimate, qi_terms = pl.pallas_call(
        back_kernel,
        grid=(count,),
        out_shape=(
            jax.ShapeDtypeStruct((count, taper_count, rows, LANES), f32),
            jax.ShapeDtypeStruct((count, rows, LANES), f32),
            jax.ShapeDtypeStruct((count, terms, LANES, rows), f32),
        ),
        in_specs=[
            smem(),
            smem(),
            smem(),
            each((shards, 2, 1, taper_count, sub_rows, LANES), 2),
            whole((2, 2 * rows, 2 * rows)),
            whole((2, 2 * LANES, 2 * LANES)),
            whole((2, rows, LANES)),
        ],
        out_specs=(
            each((1, taper_count, rows, LANES), 0),
            each(plane, 0),
            each((1, terms, LANES, rows), 0),
        ),
        scratch_shapes=[
            pltpu.VMEM((2, taper_count, rows, LANES), f32),
            pltpu.VMEM((terms, rows, LANES), f32),
        ],
    )(
        concentration, pairs, variance, recv, complex_table(rows, True), complex_table(LANES, False), inner
    )
    for sweep in range(1, ITERS):
        variance = lax.psum(jnp.sum(estimate, axis=(1, 2)), "af") / length_all
        last = sweep == ITERS - 1
        shape = flat if last else plane
        estimate = pl.pallas_call(
            functools.partial(sweep_kernel, last),
            grid=(count,),
            out_shape=jax.ShapeDtypeStruct((count,) + shape[1:], f32),
            in_specs=[smem(), smem(), each((1, taper_count, rows, LANES), 0), each(plane, 0)],
            out_specs=each(shape, 0),
            scratch_shapes=[pltpu.VMEM((rows, LANES), f32)],
        )(concentration, variance, powers, estimate)
    return (
        estimate.reshape(count, 1, local_len),
        qi_terms.reshape(count, terms, 1, local_len),
    )


def solution(mesh):
    placed = (P("sa", "af"), P(None, "af"), P(), P())
    return jax.shard_map(
        local,
        mesh=mesh,
        in_specs=placed,
        out_specs=(P("sa", "af", None), P("sa", None, "af", None)),
        check_vma=False,
    )
```

time: 608 us -> 304 us (0.50); the launches traced: 599 us -> 303 us
  matrix products: 208 us -> 0 us
  waiting for transfers between devices: 116 us -> 21.1 us
  local copies, waits for them, and re-layouts: 95.8 us -> 3.18 us
  blocking collectives: 122 us -> 211 us
  Pallas kernels: 0 us -> 44.3 us
  starting transfers between devices: 30.2 us -> 14 us
  other arithmetic: 24.1 us -> 8.28 us
    dot_general x18 -> x0, matrix products: 208 us -> none  [the longest x4 35.9 us: local(): jnp.einsum('jk,skf->sjf', qi_weights[term_index], spec_im, precision=high...]
    all_to_all x4 -> x2, waiting for transfers between devices: 116 us -> 21.1 us  [the longest x1 21 us: local(): got = lax.all_to_all(both, 'af', split_axis=0, concat_axis=0, tiled=True)]
    psum x3, blocking collectives: 122 us -> 211 us  [the longest x1 122 us: local(): variance = lax.psum(0.5 * (first + second), 'af')]
    pallas_call x0 -> x4, Pallas kernels: none -> 44.3 us  [the longest x1 31 us: local(): pl.pallas_call(back_kernel, grid=(count,), out_shape=(jax.ShapeDtypeStruc...]
    reshape x5 -> x0, local copies, waits for them, and re-layouts: 34.3 us -> none  [the longest x1 16.1 us: local(): spec_im = spec_im.reshape(series_count, taper_count, local_len)]
    reduce_sum x10 -> x0, local copies, waits for them, and re-layouts: 23 us -> none  [local(): estimate = jnp.sum(weight * powers, axis=1) / jnp.sum(weight, axis=1)]
    all_to_all x4 -> x2, starting transfers between devices: 30.2 us -> 14 us  [the longest x1 8.34 us: local(): got = lax.all_to_all(both, 'af', split_axis=0, concat_axis=0, tiled=True)]
    reduce_sum x9 -> x3, other arithmetic: 18.3 us -> 2.91 us  [the longest x2 2.15 us: local(): variance = lax.psum(jnp.sum(estimate, axis=(1, 2)), 'af') / length_all]
  transfers between devices with their start and end apart: 4 -> 2, of which waited for: 4 -> 1; matrix products, arithmetic and copies ran while one was open for 3% -> 1% of each run, Pallas kernels for 0% -> 0%
where the time goes in v1:
time: 304 us; the launch traced here: 303 us
  blocking collectives  211 us (69%)
  Pallas kernels  44.3 us (15%)
  waiting for transfers between devices  21.1 us (7%)
  starting transfers between devices  14 us (5%)
  other arithmetic  8.28 us (3%)
  local copies, waits for them, and re-layouts  3.18 us (1%)
    psum x1, blocking collectives, local(): variance = lax.psum(0.5 * (first + second), 'af')  122 us
    psum x2, blocking collectives, local(): variance = lax.psum(jnp.sum(estimate, axis=(1, 2)), 'af') / length_all  89.6 us
    pallas_call x1, Pallas kernels, local(): pl.pallas_call(back_kernel, grid=(count,), out_shape=(jax.ShapeDtypeStruc...  31 us
    all_to_all x1, waiting for transfers between devices, local(): got = lax.all_to_all(both, 'af', split_axis=0, concat_axis=0, tiled=True)  21 us
    pallas_call x2, Pallas kernels, local(): pl.pallas_call(functools.partial(sweep_kernel, last), grid=(count,), out_...  8.37 us
    all_to_all x1, starting transfers between devices, local(): got = lax.all_to_all(both, 'af', split_axis=0, concat_axis=0, tiled=True)  8.34 us
  transfers between devices with their start and end apart: 2, of which 1 were waited for; matrix products, arithmetic and copies ran while one was open for 1% of the time, Pallas kernels for 0%

profile of v1, /device:TPU:0, one launch (start us, length us, event | category | flops | bytes accessed | tf_op | source)
XLA Modules:
  0.0 302.8 jit_solution(288702936518985321)
XLA Ops:
  0.6 1.0 broadcast_multiply_fusion
  1.6 1.4 pad_maximum_fusion
  3.0 0.2 copy.125
  3.2 1.0 copy_bitcast_fusion
  4.2 8.3 %all-to-all-start = ((f32[16,14,8,128]{3,2,1,0:T(8,128)}), f32[16,14,8,128]{3,2,1,0:T(8,128)S(1)}, u32[]{:S(2)}, u32[]{:S(2)}) async-start(f32[16,14,8,128]{3,2,1,0:T(8,128)} %copy_bitcast_fusion), calls=%async_computation | async-start | bytes 1835008 | tf_op jit(solution)/shard_map/all_to_all | solution.py:191
  12.6 0.3 fusion.15
  12.8 0.6 pad_maximum_fusion.1.twist_ref
  13.5 21.0 %all-to-all-done = f32[16,14,8,128]{3,2,1,0:T(8,128)S(1)} async-done(((f32[16,14,8,128]{3,2,1,0:T(8,128)}), f32[16,14,8,128]{3,2,1,0:T(8,128)S(1)}, u32[]{:S(2)}, u32[]{:S(2)}) %all-to-all-start) | async-done | bytes 917536 | tf_op jit(solution)/shard_map/all_to_all | solution.py:191
  34.5 0.9 slice.286.tapers_ref
  35.4 0.8 multiply_reduce_fusion
  36.2 5.0 %shard_map.77 = f32[16,2,4,10,8,128]{5,4,3,2,1,0:T(8,128)} custom-call(f32[16,4,8,128]{3,2,1,0:T(8,128)} %get-tuple-element.14.series_ref, f32[16,10,8,128]{3,2,1,0:T(8,128)} %slice.286.tapers_ref, f32[2,16,8,128]{3,2,1,0:T(8,128)} %pad_maximum_fusion.1.twist_ref), custom_call_target="tpu_custom_call" | custom-call | tf_op jit(solution)/shard_map/pallas_call | solution.py:201
  41.2 0.0 copy-start
  41.2 5.7 %all-to-all-start.1 = ((f32[16,2,4,10,8,128]{5,4,3,2,1,0:T(8,128)}), f32[16,2,4,10,8,128]{5,4,3,2,1,0:T(8,128)}, u32[]{:S(2)}, u32[]{:S(2)}) async-start(f32[16,2,4,10,8,128]{5,4,3,2,1,0:T(8,128)} %shard_map.77), calls=%async_computation.1 | async-start | bytes 10485760 | tf_op jit(solution)/shard_map/all_to_all | solution.py:212
  46.8 0.0 copy-done
  46.9 0.1 copy.66
  47.0 0.3 fusion.12
  47.2 0.7 pad_maximum_fusion.2.inner_ref
  47.9 0.1 slice_bitcast_fusion.41
  48.0 0.1 slice_bitcast_fusion.3
  48.1 0.1 slice_bitcast_fusion.22
  48.2 0.7 stack.31.pair_ref
  48.9 121.6 %psum.21.var_ref = f32[4]{0:T(128)} all-reduce(f32[4]{0:T(128)S(1)} %add_multiply_fusion), channel_id=1, replica_groups=mesh['af'=16,'sa'=2] {'af'}, use_global_device_ids=true, to_apply=%region_2.0 | all-reduce | flops 4 | bytes 32 | tf_op jit(solution)/shard_map/psum | solution.py:196
  170.5 0.0 all-to-all-done.1.recv_ref
  170.5 31.0 %shard_map.78 = (f32[4,10,128,128]{3,2,1,0:T(8,128)}, f32[4,128,128]{2,1,0:T(8,128)}, f32[4,4,128,128]{3,2,1,0:T(8,128)}) custom-call(f32[10]{0:T(128)} %keep_ref.5, f32[4,55]{1,0:T(4,128)} %stack.31.pair_ref, f32[4]{0:T(128)} %psum.21.var_ref, f32[16,2,4,10,8,128]{5,4,3,2,1,0:T(8,128)} %all-to-all-done.1.recv_ref, bf16[2,256,256]{2,1,0:T(8,128)(2,1)} %constant.65.left_ref, ...), custom_call_target="tpu_custom_call" | custom-call | tf_op jit(solution)/shard_map/pallas_call | solution.py:230
  201.5 1.1 reduce_sum.38
  202.6 53.1 %psum.22 = f32[4]{0:T(128)S(1)} all-reduce(f32[4]{0:T(128)S(1)} %reduce_sum.38), channel_id=1, replica_groups=mesh['af'=16,'sa'=2] {'af'}, use_global_device_ids=true, to_apply=%region_4.5 | all-reduce | flops 4 | bytes 32 | tf_op jit(solution)/shard_map/psum | solution.py:260
  255.6 0.6 broadcast_multiply_fusion.2.var_ref
  256.2 4.1 %shard_map.79.est_ref = f32[4,128,128]{2,1,0:T(8,128)} custom-call(f32[10]{0:T(128)} %keep_ref.5, f32[4]{0:T(128)} %broadcast_multiply_fusion.2.var_ref, f32[4,10,128,128]{3,2,1,0:T(8,128)} %get-tuple-element.6.power_ref, f32[4,128,128]{2,1,0:T(8,128)} %get-tuple-element.5.est_ref), custom_call_target="tpu_custom_call" | custom-call | tf_op jit(solution)/shard_map/pallas_call | solution.py:263
  260.3 1.1 reduce_sum.39
  261.4 36.5 %psum.23 = f32[4]{0:T(128)S(1)} all-reduce(f32[4]{0:T(128)S(1)} %reduce_sum.39), channel_id=1, replica_groups=mesh['af'=16,'sa'=2] {'af'}, use_global_device_ids=true, to_apply=%region_6.7 | all-reduce | flops 4 | bytes 32 | tf_op jit(solution)/shard_map/psum | solution.py:260
  297.9 0.6 broadcast_multiply_fusion.1.var_ref
  298.5 4.3 %shard_map.80 = f32[4,128,128]{2,1,0:T(8,128)} custom-call(f32[10]{0:T(128)} %keep_ref.5, f32[4]{0:T(128)} %broadcast_multiply_fusion.1.var_ref, f32[4,10,128,128]{3,2,1,0:T(8,128)} %get-tuple-element.6.power_ref, f32[4,128,128]{2,1,0:T(8,128)} %shard_map.79.est_ref), custom_call_target="tpu_custom_call" | custom-call | tf_op jit(solution)/shard_map/pallas_call | solution.py:263
  (4 shorter events, 0.0 us)
Async XLA Ops:
  4.2 30.3 %all-to-all-start = ((f32[16,14,8,128]{3,2,1,0:T(8,128)}), f32[16,14,8,128]{3,2,1,0:T(8,128)S(1)}, u32[]{:S(2)}, u32[]{:S(2)}) async-start(f32[16,14,8,128]{3,2,1,0:T(8,128)} %copy_bitcast_fusion), calls=%async_computation | async-start | bytes 1835008 | tf_op jit(solution)/shard_map/all_to_all | solution.py:191
  41.2 5.7 %copy-start = (f32[4,10,10]{2,0,1:T(4,128)S(1)}, f32[4,10,10]{2,0,1:T(4,128)}, u32[]{:S(2)}) copy-start(f32[4,10,10]{2,0,1:T(4,128)} %param.9) | copy-start | bytes 4804
  41.2 129.3 %all-to-all-start.1 = ((f32[16,2,4,10,8,128]{5,4,3,2,1,0:T(8,128)}), f32[16,2,4,10,8,128]{5,4,3,2,1,0:T(8,128)}, u32[]{:S(2)}, u32[]{:S(2)}) async-start(f32[16,2,4,10,8,128]{5,4,3,2,1,0:T(8,128)} %shard_map.77), calls=%async_computation.1 | async-start | bytes 10485760 | tf_op jit(solution)/shard_map/all_to_all | solution.py:212

commit v2 on v1

--- a/solution.py
+++ b/solution.py
@@ -186,14 +186,14 @@
     length_all = local_len * shards
     f32 = jnp.float32
 
-    both = jnp.concatenate([series * (1.0 / math.sqrt(length_all)), tapers], axis=0)
-    both = both.reshape(count + taper_count, shards, sub_rows, LANES).transpose(1, 0, 2, 3)
+    scaled = series * (1.0 / math.sqrt(length_all))
+    energy = 0.5 * jnp.sum((scaled * tapers[:1]) ** 2 + (scaled * tapers[1:2]) ** 2, axis=1)
+    energy_row = jnp.tile(jnp.pad(energy, (0, LANES - count)), rows)[None]
+    both = jnp.concatenate([scaled, tapers, energy_row], axis=0)
+    both = both.reshape(count + taper_count + 1, shards, sub_rows, LANES).transpose(1, 0, 2, 3)
     got = lax.all_to_all(both, "af", split_axis=0, concat_axis=0, tiled=True)
-    got_series, got_tapers = got[:, :count], got[:, count:]
-
-    first = jnp.sum((got_series * got_tapers[:, :1]) ** 2, axis=(0, 2, 3))
-    second = jnp.sum((got_series * got_tapers[:, 1:2]) ** 2, axis=(0, 2, 3))
-    variance = lax.psum(0.5 * (first + second), "af")
+    got_series, got_tapers = got[:, :count], got[:, count:-1]
+    variance = jnp.sum(got[:, -1, 0, :count], axis=0)
 
     pos = rank * block_len + jnp.arange(block_len, dtype=jnp.int32)
     twist = phase(jnp.arange(shards, dtype=jnp.int32)[:, None], pos[None, :], length_all)
@@ -257,7 +257,8 @@
         concentration, pairs, variance, recv, complex_table(rows, True), complex_table(LANES, False), inner
     )
     for sweep in range(1, ITERS):
-        variance = lax.psum(jnp.sum(estimate, axis=(1, 2)), "af") / length_all
+        sums = lax.all_gather(jnp.sum(estimate, axis=(1, 2)), "af")
+        variance = jnp.sum(sums, axis=0) / length_all
         last = sweep == ITERS - 1
         shape = flat if last else plane
         estimate = pl.pallas_call(

time: 304 us -> 285 us (0.938)
  blocking collectives: 211 us -> 95.3 us
  waiting for transfers between devices: 21.1 us -> 114 us
    psum x3 -> x0, blocking collectives: 211 us -> none  [the longest x1 122 us: local(): variance = lax.psum(0.5 * (first + second), 'af')]
    unnamed x0 -> x2, blocking collectives: none -> 95.3 us
    all_to_all x1, waiting for transfers between devices: 0.01 us -> 92.2 us  [local(): recv = lax.all_to_all(turned, 'af', split_axis=0, concat_axis=0, tiled=True)]
  transfers between devices with their start and end apart: 2 -> 2, of which waited for: 1 -> 2; matrix products, arithmetic and copies ran while one was open for 1% -> 1% of each run, Pallas kernels for 0% -> 0%
where the time goes in v2:
time: 285 us; the launch traced here: 284 us
  waiting for transfers between devices  114 us (40%)
  blocking collectives  95.3 us (33%)
  Pallas kernels  44.3 us (16%)
  starting transfers between devices  14.3 us (5%)
  other arithmetic  9.27 us (3%)
  local copies, waits for them, and re-layouts  5.43 us (2%)
    unnamed x2, blocking collectives  95.3 us
    all_to_all x1, waiting for transfers between devices, local(): recv = lax.all_to_all(turned, 'af', split_axis=0, concat_axis=0, tiled=True)  92.2 us
    pallas_call x1, Pallas kernels, local(): pl.pallas_call(back_kernel, grid=(count,), out_shape=(jax.ShapeDtypeStruc...  30.9 us
    all_to_all x1, waiting for transfers between devices, local(): got = lax.all_to_all(both, 'af', split_axis=0, concat_axis=0, tiled=True)  22.2 us
    pallas_call x2, Pallas kernels, local(): pl.pallas_call(functools.partial(sweep_kernel, last), grid=(count,), out_...  8.37 us
    all_to_all x1, starting transfers between devices, local(): got = lax.all_to_all(both, 'af', split_axis=0, concat_axis=0, tiled=True)  8.34 us
    all_to_all x1, starting transfers between devices, local(): recv = lax.all_to_all(turned, 'af', split_axis=0, concat_axis=0, tiled=True)  5.92 us
  transfers between devices with their start and end apart: 2, of which 2 were waited for; matrix products, arithmetic and copies ran while one was open for 1% of the time, Pallas kernels for 0%

profile of v2, /device:TPU:0, one launch (start us, length us, event | category | flops | bytes accessed | tf_op | source)
XLA Modules:
  0.0 284.5 jit_solution(16552296311364218025)
XLA Ops:
  0.6 1.3 slice_multiply_fusion.1
  1.9 1.2 multiply_bitcast_fusion
  3.2 1.4 copy.127
  4.7 1.0 maximum_bitcast_fusion
  5.7 8.3 %all-to-all-start = ((f32[16,15,8,128]{3,2,1,0:T(8,128)}), f32[16,15,8,128]{3,2,1,0:T(8,128)S(1)}, u32[]{:S(2)}, u32[]{:S(2)}) async-start(f32[16,15,8,128]{3,2,1,0:T(8,128)} %maximum_bitcast_fusion), calls=%async_computation | async-start | bytes 1966080 | tf_op jit(solution)/shard_map/all_to_all | solution.py:194
  14.0 0.3 fusion.15
  14.3 0.6 pad_maximum_fusion.twist_ref
  15.0 22.2 %all-to-all-done = f32[16,15,8,128]{3,2,1,0:T(8,128)S(1)} async-done(((f32[16,15,8,128]{3,2,1,0:T(8,128)}), f32[16,15,8,128]{3,2,1,0:T(8,128)S(1)}, u32[]{:S(2)}, u32[]{:S(2)}) %all-to-all-start) | async-done | bytes 983072 | tf_op jit(solution)/shard_map/all_to_all | solution.py:194
  37.1 0.7 slice.286.series_ref
  37.9 0.9 slice.287.tapers_ref
  38.8 5.0 %shard_map.77 = f32[16,2,4,10,8,128]{5,4,3,2,1,0:T(8,128)} custom-call(f32[16,4,8,128]{3,2,1,0:T(8,128)} %slice.286.series_ref, f32[16,10,8,128]{3,2,1,0:T(8,128)} %slice.287.tapers_ref, f32[2,16,8,128]{3,2,1,0:T(8,128)} %pad_maximum_fusion.twist_ref), custom_call_target="tpu_custom_call" | custom-call | tf_op jit(solution)/shard_map/pallas_call | solution.py:201
  43.8 0.0 copy-start
  43.8 0.0 copy-start.1
  43.8 5.9 %all-to-all-start.1 = ((f32[16,2,4,10,8,128]{5,4,3,2,1,0:T(8,128)}), f32[16,2,4,10,8,128]{5,4,3,2,1,0:T(8,128)}, u32[]{:S(2)}, u32[]{:S(2)}) async-start(f32[16,2,4,10,8,128]{5,4,3,2,1,0:T(8,128)} %shard_map.77), calls=%async_computation.1 | async-start | bytes 10485760 | tf_op jit(solution)/shard_map/all_to_all | solution.py:212
  49.7 0.0 copy-done
  49.7 0.1 copy.66
  49.8 0.0 copy-done.1
  49.8 0.6 dynamic-slice
  51.1 0.1 slice_bitcast_fusion.39
  51.2 0.1 slice_bitcast_fusion.20
  51.3 0.1 slice_bitcast_fusion.1
  51.4 0.8 stack.31.pair_ref
  52.1 0.3 fusion.12
  52.4 0.7 pad_maximum_fusion.1.inner_ref
  53.0 0.5 slice_reduce_fusion.var_ref
  53.6 92.2 %all-to-all-done.1.recv_ref = f32[16,2,4,10,8,128]{5,4,3,2,1,0:T(8,128)} async-done(((f32[16,2,4,10,8,128]{5,4,3,2,1,0:T(8,128)}), f32[16,2,4,10,8,128]{5,4,3,2,1,0:T(8,128)}, u32[]{:S(2)}, u32[]{:S(2)}) %all-to-all-start.1) | async-done | bytes 5242912 | tf_op jit(solution)/shard_map/all_to_all | solution.py:212
  145.8 30.9 %shard_map.78 = (f32[4,10,128,128]{3,2,1,0:T(8,128)}, f32[4,128,128]{2,1,0:T(8,128)}, f32[4,4,128,128]{3,2,1,0:T(8,128)}) custom-call(f32[10]{0:T(128)} %keep_ref.5, f32[4,55]{1,0:T(4,128)} %stack.31.pair_ref, f32[4]{0:T(128)} %slice_reduce_fusion.var_ref, f32[16,2,4,10,8,128]{5,4,3,2,1,0:T(8,128)} %all-to-all-done.1.recv_ref, ...), custom_call_target="tpu_custom_call" | custom-call | tf_op jit(solution)/shard_map/pallas_call | solution.py:230
  176.8 1.1 reduce_sum.56
  177.8 0.2 dynamic-update-slice
  178.1 58.8 %all-reduce.1 = f32[64]{0:T(128)S(1)} all-reduce(f32[64]{0:T(128)S(1)} %dynamic-update-slice), channel_id=2, replica_groups=mesh['af'=16,'sa'=2] {'af'}, use_global_device_ids=true, to_apply=%add.1 | all-reduce | flops 64 | bytes 512
  236.9 0.1 reshape.180
  237.0 0.6 broadcast_multiply_fusion.1.var_ref
  237.5 4.1 %shard_map.79.est_ref = f32[4,128,128]{2,1,0:T(8,128)} custom-call(f32[10]{0:T(128)} %keep_ref.5, f32[4]{0:T(128)} %broadcast_multiply_fusion.1.var_ref, f32[4,10,128,128]{3,2,1,0:T(8,128)} %get-tuple-element.6.power_ref, f32[4,128,128]{2,1,0:T(8,128)} %get-tuple-element.5.est_ref), custom_call_target="tpu_custom_call" | custom-call | tf_op jit(solution)/shard_map/pallas_call | solution.py:264
  241.6 1.1 reduce_sum.58
  242.7 0.2 dynamic-update-slice.1
  242.9 36.5 %all-reduce.2 = f32[64]{0:T(128)S(1)} all-reduce(f32[64]{0:T(128)S(1)} %dynamic-update-slice.1), channel_id=3, replica_groups=mesh['af'=16,'sa'=2] {'af'}, use_global_device_ids=true, to_apply=%add.2 | all-reduce | flops 64 | bytes 512
  279.5 0.1 reshape.181
  279.6 0.6 broadcast_multiply_fusion.var_ref
  280.2 4.3 %shard_map.80 = f32[4,128,128]{2,1,0:T(8,128)} custom-call(f32[10]{0:T(128)} %keep_ref.5, f32[4]{0:T(128)} %broadcast_multiply_fusion.var_ref, f32[4,10,128,128]{3,2,1,0:T(8,128)} %get-tuple-element.6.power_ref, f32[4,128,128]{2,1,0:T(8,128)} %shard_map.79.est_ref), custom_call_target="tpu_custom_call" | custom-call | tf_op jit(solution)/shard_map/pallas_call | solution.py:264
  (10 shorter events, 0.1 us)
Async XLA Ops:
  5.7 31.5 %all-to-all-start = ((f32[16,15,8,128]{3,2,1,0:T(8,128)}), f32[16,15,8,128]{3,2,1,0:T(8,128)S(1)}, u32[]{:S(2)}, u32[]{:S(2)}) async-start(f32[16,15,8,128]{3,2,1,0:T(8,128)} %maximum_bitcast_fusion), calls=%async_computation | async-start | bytes 1966080 | tf_op jit(solution)/shard_map/all_to_all | solution.py:194
  43.8 5.9 %copy-start = (f32[4,10,10]{2,0,1:T(4,128)S(1)}, f32[4,10,10]{2,0,1:T(4,128)}, u32[]{:S(2)}) copy-start(f32[4,10,10]{2,0,1:T(4,128)} %param.9) | copy-start | bytes 4804
  43.8 6.1 %copy-start.1 = (u32[32]{0:T(128)S(1)}, u32[32]{0:T(128)}, u32[]{:S(2)}) copy-start(u32[32]{0:T(128)} %constant.79) | copy-start | bytes 388
  43.8 102.0 %all-to-all-start.1 = ((f32[16,2,4,10,8,128]{5,4,3,2,1,0:T(8,128)}), f32[16,2,4,10,8,128]{5,4,3,2,1,0:T(8,128)}, u32[]{:S(2)}, u32[]{:S(2)}) async-start(f32[16,2,4,10,8,128]{5,4,3,2,1,0:T(8,128)} %shard_map.77), calls=%async_computation.1 | async-start | bytes 10485760 | tf_op jit(solution)/shard_map/all_to_all | solution.py:212

commit v3 on v2

--- a/solution.py
+++ b/solution.py
@@ -149,6 +149,51 @@
     out_ref[0] = hold[...].T if last else hold[...]
 
 
+def total_kernel(part_ref, out_ref, slots, send_sem, recv_sem):
+    shards = slots.shape[0]
+    me = lax.axis_index("af")
+    barrier = pltpu.get_barrier_semaphore()
+    peers = [lax.rem(me + d, shards) for d in range(shards)]
+    for peer in peers[1:]:
+        pl.semaphore_signal(
+            barrier, inc=1, device_id={"af": peer}, device_id_type=pl.DeviceIdType.MESH
+        )
+    pl.semaphore_wait(barrier, shards - 1)
+    copies = []
+    for d in range(1, shards):
+        copy = pltpu.make_async_remote_copy(
+            src_ref=part_ref,
+            dst_ref=slots.at[d],
+            send_sem=send_sem.at[d],
+            recv_sem=recv_sem.at[d],
+            device_id={"af": peers[d]},
+            device_id_type=pl.DeviceIdType.MESH,
+        )
+        copy.start()
+        copies.append(copy)
+    total = part_ref[...]
+    for d, copy in enumerate(copies, 1):
+        copy.wait()
+        total += slots[d]
+    out_ref[...] = total
+
+
+def total_over_devices(part, shards, ident):
+    vmem = pl.BlockSpec(memory_space=pltpu.VMEM)
+    return pl.pallas_call(
+        total_kernel,
+        out_shape=jax.ShapeDtypeStruct(part.shape, part.dtype),
+        in_specs=[vmem],
+        out_specs=vmem,
+        scratch_shapes=[
+            pltpu.VMEM((shards,) + part.shape, part.dtype),
+            pltpu.SemaphoreType.DMA((shards,)),
+            pltpu.SemaphoreType.DMA((shards,)),
+        ],
+        compiler_params=pltpu.CompilerParams(collective_id=ident, has_side_effects=True),
+    )(part)
+
+
 def whole(shape):
     return pl.BlockSpec(shape, lambda i: (0,) * len(shape))
 
@@ -257,8 +302,8 @@
         concentration, pairs, variance, recv, complex_table(rows, True), complex_table(LANES, False), inner
     )
     for sweep in range(1, ITERS):
-        sums = lax.all_gather(jnp.sum(estimate, axis=(1, 2)), "af")
-        variance = jnp.sum(sums, axis=0) / length_all
+        sums = total_over_devices(jnp.sum(estimate, axis=1), shards, sweep)
+        variance = jnp.sum(sums, axis=1) / length_all
         last = sweep == ITERS - 1
         shape = flat if last else plane
         estimate = pl.pallas_call(

time: 285 us -> 228 us (0.80)
  blocking collectives: 95.3 us -> 0 us
  Pallas kernels: 44.3 us -> 81 us
    unnamed x2 -> x0, blocking collectives: 95.3 us -> none
    pallas_call x0 -> x2, Pallas kernels: none -> 36.7 us  [total_over_devices(): pl.pallas_call(total_kernel, out_shape=jax.ShapeDtypeStruct(part.shape, p...]
  transfers between devices with their start and end apart: 2 -> 2, of which waited for: 2 -> 2; matrix products, arithmetic and copies ran while one was open for 1% -> 2% of each run, Pallas kernels for 0% -> 0%
where the time goes in v3:
time: 228 us
  waiting for transfers between devices  116 us (51%)
  Pallas kernels  81 us (36%)
  starting transfers between devices  14.3 us (6%)
  other arithmetic  11.8 us (5%)
  local copies, waits for them, and re-layouts  4.21 us (2%)
    all_to_all x1, waiting for transfers between devices, local(): recv = lax.all_to_all(turned, 'af', split_axis=0, concat_axis=0, tiled=True)  93.5 us
    pallas_call x2, Pallas kernels, total_over_devices(): pl.pallas_call(total_kernel, out_shape=jax.ShapeDtypeStruct(part.shape, p...  36.7 us
    pallas_call x1, Pallas kernels, local(): pl.pallas_call(back_kernel, grid=(count,), out_shape=(jax.ShapeDtypeStruc...  30.9 us
    all_to_all x1, waiting for transfers between devices, local(): got = lax.all_to_all(both, 'af', split_axis=0, concat_axis=0, tiled=True)  22.2 us
    pallas_call x2, Pallas kernels, local(): pl.pallas_call(functools.partial(sweep_kernel, last), grid=(count,), out_...  8.37 us
    all_to_all x1, starting transfers between devices, local(): got = lax.all_to_all(both, 'af', split_axis=0, concat_axis=0, tiled=True)  8.34 us
    all_to_all x1, starting transfers between devices, local(): recv = lax.all_to_all(turned, 'af', split_axis=0, concat_axis=0, tiled=True)  5.92 us
    pallas_call x1, Pallas kernels, local(): pl.pallas_call(front_kernel, grid=(count,), out_shape=jax.ShapeDtypeStruc...  5.02 us
  transfers between devices with their start and end apart: 2, of which 2 were waited for; matrix products, arithmetic and copies ran while one was open for 2% of the time, Pallas kernels for 0%

profile of v3, /device:TPU:0, one launch (start us, length us, event | category | flops | bytes accessed | tf_op | source)
XLA Modules:
  0.0 227.7 jit_solution(2784604995735585082)
XLA Ops:
  0.6 1.3 slice_multiply_fusion.1
  1.9 1.2 multiply_bitcast_fusion
  3.2 1.4 copy.127
  4.7 1.0 maximum_bitcast_fusion
  5.7 8.3 %all-to-all-start = ((f32[16,15,8,128]{3,2,1,0:T(8,128)}), f32[16,15,8,128]{3,2,1,0:T(8,128)S(1)}, u32[]{:S(2)}, u32[]{:S(2)}) async-start(f32[16,15,8,128]{3,2,1,0:T(8,128)} %maximum_bitcast_fusion), calls=%async_computation | async-start | bytes 1966080 | tf_op jit(solution)/shard_map/all_to_all | solution.py:239
  14.0 0.3 fusion.15
  14.3 0.6 pad_maximum_fusion.twist_ref
  15.0 22.2 %all-to-all-done = f32[16,15,8,128]{3,2,1,0:T(8,128)S(1)} async-done(((f32[16,15,8,128]{3,2,1,0:T(8,128)}), f32[16,15,8,128]{3,2,1,0:T(8,128)S(1)}, u32[]{:S(2)}, u32[]{:S(2)}) %all-to-all-start) | async-done | bytes 983072 | tf_op jit(solution)/shard_map/all_to_all | solution.py:239
  37.1 0.7 slice.286.series_ref
  37.9 0.9 slice.287.tapers_ref
  38.8 5.0 %shard_map.77 = f32[16,2,4,10,8,128]{5,4,3,2,1,0:T(8,128)} custom-call(f32[16,4,8,128]{3,2,1,0:T(8,128)} %slice.286.series_ref, f32[16,10,8,128]{3,2,1,0:T(8,128)} %slice.287.tapers_ref, f32[2,16,8,128]{3,2,1,0:T(8,128)} %pad_maximum_fusion.twist_ref), custom_call_target="tpu_custom_call" | custom-call | tf_op jit(solution)/shard_map/pallas_call | solution.py:246
  43.8 0.0 copy-start
  43.8 5.9 %all-to-all-start.1 = ((f32[16,2,4,10,8,128]{5,4,3,2,1,0:T(8,128)}), f32[16,2,4,10,8,128]{5,4,3,2,1,0:T(8,128)}, u32[]{:S(2)}, u32[]{:S(2)}) async-start(f32[16,2,4,10,8,128]{5,4,3,2,1,0:T(8,128)} %shard_map.77), calls=%async_computation.1 | async-start | bytes 10485760 | tf_op jit(solution)/shard_map/all_to_all | solution.py:257
  49.7 0.0 copy-done
  49.7 0.1 copy.66
  49.8 0.1 slice_bitcast_fusion.39
  49.9 0.1 slice_bitcast_fusion.20
  50.0 0.1 slice_bitcast_fusion.1
  50.1 0.8 stack.31.pair_ref
  50.9 0.3 fusion.12
  51.1 0.7 pad_maximum_fusion.1.inner_ref
  51.8 0.6 slice_reduce_fusion.var_ref
  52.3 93.5 %all-to-all-done.1.recv_ref = f32[16,2,4,10,8,128]{5,4,3,2,1,0:T(8,128)} async-done(((f32[16,2,4,10,8,128]{5,4,3,2,1,0:T(8,128)}), f32[16,2,4,10,8,128]{5,4,3,2,1,0:T(8,128)}, u32[]{:S(2)}, u32[]{:S(2)}) %all-to-all-start.1) | async-done | bytes 5242912 | tf_op jit(solution)/shard_map/all_to_all | solution.py:257
  145.8 30.9 %shard_map.78 = (f32[4,10,128,128]{3,2,1,0:T(8,128)}, f32[4,128,128]{2,1,0:T(8,128)}, f32[4,4,128,128]{3,2,1,0:T(8,128)}) custom-call(f32[10]{0:T(128)} %keep_ref.5, f32[4,55]{1,0:T(4,128)} %stack.31.pair_ref, f32[4]{0:T(128)} %slice_reduce_fusion.var_ref, f32[16,2,4,10,8,128]{5,4,3,2,1,0:T(8,128)} %all-to-all-done.1.recv_ref, ...), custom_call_target="tpu_custom_call" | custom-call | tf_op jit(solution)/shard_map/pallas_call | solution.py:275
  176.8 1.6 reduce_sum.56.part_ref
  178.3 27.9 %shard_map.79 = f32[4,128]{1,0:T(4,128)} custom-call(f32[4,128]{1,0:T(4,128)} %reduce_sum.56.part_ref), custom_call_target="tpu_custom_call" | custom-call | tf_op jit(solution)/shard_map/pallas_call | solution.py:183
  206.2 0.8 reduce_sum.57
  207.0 0.6 broadcast_multiply_fusion.1.var_ref
  207.6 4.1 %shard_map.80.est_ref = f32[4,128,128]{2,1,0:T(8,128)} custom-call(f32[10]{0:T(128)} %keep_ref.5, f32[4]{0:T(128)} %broadcast_multiply_fusion.1.var_ref, f32[4,10,128,128]{3,2,1,0:T(8,128)} %get-tuple-element.6.power_ref, f32[4,128,128]{2,1,0:T(8,128)} %get-tuple-element.5.est_ref), custom_call_target="tpu_custom_call" | custom-call | tf_op jit(solution)/shard_map/pallas_call | solution.py:309
  211.6 1.6 reduce_sum.58.part_ref
  213.2 8.8 %shard_map.81 = f32[4,128]{1,0:T(4,128)} custom-call(f32[4,128]{1,0:T(4,128)} %reduce_sum.58.part_ref), custom_call_target="tpu_custom_call" | custom-call | tf_op jit(solution)/shard_map/pallas_call | solution.py:183
  222.0 0.8 reduce_sum.59
  222.8 0.6 broadcast_multiply_fusion.var_ref
  223.4 4.3 %shard_map.82 = f32[4,128,128]{2,1,0:T(8,128)} custom-call(f32[10]{0:T(128)} %keep_ref.5, f32[4]{0:T(128)} %broadcast_multiply_fusion.var_ref, f32[4,10,128,128]{3,2,1,0:T(8,128)} %get-tuple-element.6.power_ref, f32[4,128,128]{2,1,0:T(8,128)} %shard_map.80.est_ref), custom_call_target="tpu_custom_call" | custom-call | tf_op jit(solution)/shard_map/pallas_call | solution.py:309
  (6 shorter events, 0.1 us)
Async XLA Ops:
  5.7 31.5 %all-to-all-start = ((f32[16,15,8,128]{3,2,1,0:T(8,128)}), f32[16,15,8,128]{3,2,1,0:T(8,128)S(1)}, u32[]{:S(2)}, u32[]{:S(2)}) async-start(f32[16,15,8,128]{3,2,1,0:T(8,128)} %maximum_bitcast_fusion), calls=%async_computation | async-start | bytes 1966080 | tf_op jit(solution)/shard_map/all_to_all | solution.py:239
  43.8 5.9 %copy-start = (f32[4,10,10]{2,0,1:T(4,128)S(1)}, f32[4,10,10]{2,0,1:T(4,128)}, u32[]{:S(2)}) copy-start(f32[4,10,10]{2,0,1:T(4,128)} %param.9) | copy-start | bytes 4804
  43.8 102.0 %all-to-all-start.1 = ((f32[16,2,4,10,8,128]{5,4,3,2,1,0:T(8,128)}), f32[16,2,4,10,8,128]{5,4,3,2,1,0:T(8,128)}, u32[]{:S(2)}, u32[]{:S(2)}) async-start(f32[16,2,4,10,8,128]{5,4,3,2,1,0:T(8,128)} %shard_map.77), calls=%async_computation.1 | async-start | bytes 10485760 | tf_op jit(solution)/shard_map/all_to_all | solution.py:257
